TPU v7x, 32 devices: a whole 2x2x4 slice. The times are simulated.
32 devices in a mesh: grp: 4 (over y, core), blk: 8 (over z, x).
Axes of the slice: x: 2, y: 2, z: 4, core: 2. Of those that a mesh axis runs over, the one named last changes fastest.
Arguments:
- embeds: bfloat16 [4, 8192, 1024], P('grp', 'blk')
- doc_ids: int32 [4, 8192], P('grp', 'blk'), may hold values from 0 to 8191, each once within a row
- prior_max: float32 [4, 8192], P('grp', 'blk'), may hold values from -0.2 to 0.6
- owned: bfloat16 [2048, 1024], P(('grp', 'blk')), may hold values from -6 to 6
- owned_ids: int32 [2048], P(('grp', 'blk')), may hold values from 0 to 2047, each once
- owner_dest: int32 [2048, 1], P(('grp', 'blk')), may hold values from 0 to 31; in each aligned block of 64 rows (0 to 63, 64 to 127, ...) at most 4 rows name the same one
Outputs:
- running_max: float32 [4, 8192], P('grp', 'blk')
- next_rows: bfloat16 [4096, 1024], P(('grp', 'blk'))
- next_ids: int32 [4096], P(('grp', 'blk'))
Inputs may be any that keep to these rules, and one draw needn't show every extreme that they name: `owner_dest`: among the 64 rows of one device no target is named more than 4 times, a bound that some block reaches.
All inputs are finite; a program needn't handle non-finite values.
Results may differ from a plain program's by a relative error of at most 0.0016.
Values may be sent and summed in bfloat16 or wider, within the bound.
A program may use at most 64 MiB of HBM per device.

v0:
```python
import functools

import jax
import jax.numpy as jnp
from jax import lax
from jax.experimental import pallas as pl
from jax.experimental.pallas import tpu as pltpu
from jax.sharding import PartitionSpec as P

CYCLE = 3
CAP = 4
CHUNKS = 4
LANES = 128
EMPTY = -2.0


def make_plan(nz):
    if nz == 4:
        received = [[], [(0, 0)], [(1, 1), (0, 1), (3, 3)], [(1, 2), (0, 2)]]
        late = [z == 3 for z in range(nz)]
    else:
        received = [[((z - 1) % nz, (z - 1) % nz), ((z - 2) % nz, (z - 1) % nz)] for z in range(nz)]
        late = [False] * nz
    own_to = [(-1, 0)] * nz
    forward = [[(-1, 0)] * len(received[z]) for z in range(nz)]
    rank = [[0] * len(received[z]) for z in range(nz)]
    returns = [0] * nz
    for z in range(nz):
        for slot, (block, source) in enumerate(received[z]):
            if block == source:
                own_to[source] = (z, slot)
            else:
                held = [entry[0] for entry in received[source]].index(block)
                forward[source][held] = (z, slot)
            rank[z][slot] = returns[block]
            returns[block] += 1
    return received, own_to, late, forward, rank, returns


def pick(index, values):
    result = jnp.int32(values[0])
    for i in range(1, len(values)):
        if values[i] != values[0]:
            result = jnp.where(index == i, jnp.int32(values[i]), result)
    return result


def kernel(plan, sizes, emb, ids, prior, owned, owned_ids, dest,
           run_out, rows_out, ids_out,
           raw, nrm, idv, idt, acc, ret, obuf, oid,
           local_sem, send_sem, recv_sem, ids_send, ids_recv, ret_send, ret_recv,
           rows_send, rows_recv, oids_send, oids_recv, keep_sem):
    n_grp, n_blk = sizes
    devices = n_grp * n_blk
    nz = n_blk // 2
    received, own_to, late, forward, rank, returns = plan
    slots = max(len(entry) for entry in received)
    rows = emb.shape[1]
    ch = rows // CHUNKS
    g = lax.axis_index("grp")
    b = lax.axis_index("blk")
    flip = g % 2
    z = b // 2
    x = b % 2
    role = z + flip * (nz - 1 - 2 * z)

    def block_of(zr):
        return 2 * (zr + flip * (nz - 1 - 2 * zr)) + x

    partner = b + 1 - 2 * x

    def table(values, slot=None, empty=0):
        if slot is None:
            return pick(role, values)
        return pick(role, [v[slot] if slot < len(v) else empty for v in values])

    own_z, own_slot = table([v[0] for v in own_to]), table([v[1] for v in own_to])
    is_late = table([int(v) for v in late])
    exists = [table([[1] * len(v) for v in received], s) for s in range(slots)]
    slot_z = [table([[e[0] for e in v] for v in received], s) for s in range(slots)]
    fwd_z = [table([[e[0] for e in v] for v in forward], s, -1) for s in range(slots)]
    fwd_slot = [table([[e[1] for e in v] for v in forward], s) for s in range(slots)]
    ranks = [table(rank, s) for s in range(slots)]
    n_returns = table(returns)
    blocks = [b, partner] + [block_of(slot_z[s]) for s in range(slots)]

    def span(c):
        if isinstance(c, int):
            return pl.ds(c * ch, ch)
        return pl.ds(pl.multiple_of(c * ch, ch), ch)

    def remote(src, dst, ssem, rsem, blk, grp=None):
        return pltpu.make_async_remote_copy(
            src_ref=src, dst_ref=dst, send_sem=ssem, recv_sem=rsem,
            device_id=(g if grp is None else grp, blk), device_id_type=pl.DeviceIdType.MESH)

    def chunk_copy(src, lane, to_slot, blk, c):
        return remote(src, raw.at[to_slot, span(c), :], send_sem.at[lane, c], recv_sem.at[to_slot, c], blk)

    def ids_copy(src, lane, to_slot, blk):
        return remote(src, idv.at[to_slot], ids_send.at[lane], ids_recv.at[to_slot], blk)

    def own_column(c):
        return chunk_copy(emb.at[0, span(c), :], 1, 2 + own_slot, block_of(own_z), c)

    def partner_copy(c):
        return chunk_copy(emb.at[0, span(c), :], 0, 1, partner, c)

    def forward_copy(s, c):
        return chunk_copy(raw.at[2 + s, span(c), :], 2 + s, 2 + fwd_slot[s], block_of(fwd_z[s]), c)

    def start_own_column():
        ids_copy(ids, 1, 2 + own_slot, block_of(own_z)).start()
        for c in range(CHUNKS):
            own_column(c).start()

    local = pltpu.make_async_copy(emb.at[0], raw.at[0], local_sem)
    local.start()

    @pl.when((own_z >= 0) & (is_late == 0))
    def _():
        start_own_column()

    ids_copy(ids, 0, 1, partner).start()
    for c in range(CHUNKS):
        partner_copy(c).start()

    def normalize(values):
        values = values.astype(jnp.float32)
        scale = lax.rsqrt(jnp.sum(values * values, axis=-1, keepdims=True) + 1e-06)
        return (values * scale).astype(jnp.bfloat16)

    own_dev = owned.shape[0]
    owned_normed = normalize(owned[...])
    t_col = dest[...].astype(jnp.float32)
    t_row = jnp.transpose(jnp.broadcast_to(t_col, (own_dev, LANES)))[0:1, :]
    row_i = lax.broadcasted_iota(jnp.int32, (own_dev, own_dev), 0)
    col_i = lax.broadcasted_iota(jnp.int32, (own_dev, own_dev), 1)
    earlier = jnp.where((row_i < col_i) & (t_col == t_row), 1.0, 0.0)
    position = jnp.sum(earlier, axis=0, keepdims=True)
    place = t_row * CAP + position
    which = lax.broadcasted_iota(jnp.int32, (devices * CAP, own_dev), 0).astype(jnp.float32)
    onehot = jnp.where(which == place, 1.0, 0.0).astype(jnp.bfloat16)
    outgoing = jnp.dot(onehot, owned_normed, preferred_element_type=jnp.float32).astype(jnp.bfloat16)
    dev_i = lax.broadcasted_iota(jnp.int32, (devices, own_dev), 0).astype(jnp.float32)
    lane_i = lax.broadcasted_iota(jnp.int32, (devices, LANES), 1)
    number = owned_ids[...].astype(jnp.float32) + 1.0
    outgoing_ids = jnp.full((devices, LANES), -1.0, jnp.float32)
    for k in range(CAP):
        here = jnp.where((dev_i == t_row) & (position == float(k)), number, 0.0)
        found = jnp.sum(here, axis=1, keepdims=True) - 1.0
        outgoing_ids = jnp.where(lane_i == k, found, outgoing_ids)
    outgoing_ids = outgoing_ids.astype(jnp.int32)
    for d in range(devices):
        obuf[d] = outgoing[d * CAP:(d + 1) * CAP, :]
        oid[d] = outgoing_ids[d:d + 1, :]

    def ready(s, c):
        at = span(c)
        nrm[s, at, :] = normalize(raw[s, at, :])
        for p in range(ch // LANES):
            at = pl.ds(pl.multiple_of(c * ch + p * LANES, LANES), LANES)
            line = idv[s, :, at].astype(jnp.float32)
            idt[s, at, :] = jnp.transpose(jnp.broadcast_to(line, (LANES, LANES)))

    def tile(row, row_at, width, col, col_at):
        scores = lax.dot_general(
            nrm[col, col_at, :], nrm[row, row_at, :], (((1,), (1,)), ((), ())),
            preferred_element_type=jnp.float32)
        row_ids = idv[row, :, row_at].astype(jnp.float32)
        col_ids = idt[col, col_at, :]
        parts = []
        for p in range(width // LANES):
            cut = slice(p * LANES, (p + 1) * LANES)
            masked = jnp.where(col_ids < row_ids[:, cut], scores[:, cut], EMPTY)
            parts.append(jnp.max(masked, axis=0, keepdims=True))
        acc[row, :, row_at] = jnp.maximum(acc[row, :, row_at], jnp.concatenate(parts, axis=1))

    whole = pl.ds(0, rows)

    acc[0] = prior[...]
    for s in range(1, 2 + slots):
        acc[s] = jnp.full((1, rows), EMPTY, jnp.float32)
    idv[0] = ids[...]
    local.wait()

    @pl.loop(0, CHUNKS)
    def _(c):
        ready(0, c)

    me = g * n_blk + b

    def to_device(step):
        other = (me + step) % devices
        return other, other // n_blk, other % n_blk

    @pl.loop(1, devices)
    def _(step):
        other, og, ob = to_device(step)
        remote(obuf.at[other], rows_out.at[me], rows_send, rows_recv, ob, og).start()
        remote(oid.at[other], ids_out.at[me], oids_send, oids_recv, ob, og).start()

    keep_rows = pltpu.make_async_copy(obuf.at[me], rows_out.at[me], keep_sem.at[0])
    keep_ids = pltpu.make_async_copy(oid.at[me], ids_out.at[me], keep_sem.at[1])
    keep_rows.start()
    keep_ids.start()

    def is_row(u, v):
        diff = (u - v + n_blk) % n_blk
        return (diff >= 1) & (diff <= CYCLE)

    def against_whole(s, c, other):
        @pl.when(is_row(blocks[s], blocks[other]))
        def _():
            tile(s, span(c), ch, other, whole)

        @pl.when(is_row(blocks[other], blocks[s]))
        def _():
            tile(other, whole, rows, s, span(c))

    def against_part(s, c, other, count):
        @pl.when(is_row(blocks[s], blocks[other]))
        def _():
            @pl.loop(0, count)
            def _(j):
                tile(s, span(c), ch, other, span(j))

        @pl.when(is_row(blocks[other], blocks[s]))
        def _():
            @pl.loop(0, count)
            def _(j):
                tile(other, span(j), ch, s, span(c))

    def arrive(s, c):
        chunk_copy(raw.at[s, span(c), :], 0, s, partner, c).wait_recv()

        @pl.when(c == 0)
        def _():
            ids_copy(idv.at[s], 0, s, partner).wait_recv()

        if s >= 2:
            @pl.when(fwd_z[s - 2] >= 0)
            def _():
                forward_copy(s - 2, c).start()

                @pl.when(c == 0)
                def _():
                    ids_copy(idv.at[s], s, 2 + fwd_slot[s - 2], block_of(fwd_z[s - 2])).start()

    @pl.loop(0, CHUNKS)
    def _(c):
        tile(0, whole, rows, 0, span(c))

    @pl.loop(0, CHUNKS)
    def _(c):
        @pl.when(exists[0] == 1)
        def _():
            arrive(2, c)
            ready(2, c)
            against_whole(2, c, 0)

    @pl.when((own_z >= 0) & (is_late == 1))
    def _():
        start_own_column()

    @pl.loop(0, CHUNKS)
    def _(c):
        for s in range(1, slots):
            @pl.when(exists[s] == 1)
            def _(s=s):
                arrive(2 + s, c)
                ready(2 + s, c)
                against_whole(2 + s, c, 0)
                against_part(2 + s, c, 1, c)

        arrive(1, c)
        ready(1, c)

        @pl.when(is_row(b, partner))
        def _():
            tile(0, whole, rows, 1, span(c))

        @pl.when(exists[0] == 1)
        def _():
            against_whole(1, c, 2)

        for s in range(1, slots):
            @pl.when(exists[s] == 1)
            def _(s=s):
                against_part(1, c, 2 + s, c + 1)

    back = remote(acc.at[1], ret.at[0], ret_send.at[0], ret_recv.at[0], partner)
    back.start()
    for s in range(slots):
        @pl.when(exists[s] == 1)
        def _(s=s):
            remote(acc.at[2 + s], ret.at[1 + ranks[s]], ret_send.at[1 + s], ret_recv.at[1 + ranks[s]],
                   block_of(slot_z[s])).start()

    for c in range(CHUNKS):
        partner_copy(c).wait_send()
    ids_copy(ids, 0, 1, partner).wait_send()

    @pl.when(own_z >= 0)
    def _():
        for c in range(CHUNKS):
            own_column(c).wait_send()
        ids_copy(ids, 1, 2 + own_slot, block_of(own_z)).wait_send()

    for s in range(slots):
        @pl.when(fwd_z[s] >= 0)
        def _(s=s):
            for c in range(CHUNKS):
                forward_copy(s, c).wait_send()
            ids_copy(idv.at[2 + s], 2 + s, 2 + fwd_slot[s], block_of(fwd_z[s])).wait_send()

    keep_rows.wait()
    keep_ids.wait()
    others = pl.ds(0, devices - 1)
    pltpu.make_async_copy(obuf.at[others], rows_out.at[others], rows_send).wait()
    pltpu.make_async_copy(oid.at[others], ids_out.at[others], oids_send).wait()
    pltpu.make_async_copy(obuf.at[others], rows_out.at[others], rows_recv).wait()
    pltpu.make_async_copy(oid.at[others], ids_out.at[others], oids_recv).wait()

    back.wait_recv()
    run_out[...] = jnp.maximum(acc[0], ret[0])
    for k in range(max(returns)):
        @pl.when(k < n_returns)
        def _(k=k):
            remote(acc.at[1], ret.at[1 + k], ret_send.at[0], ret_recv.at[1 + k], partner).wait_recv()
            run_out[...] = jnp.maximum(run_out[...], ret[1 + k])

    back.wait_send()
    for s in range(slots):
        @pl.when(exists[s] == 1)
        def _(s=s):
            remote(acc.at[2 + s], ret.at[1 + ranks[s]], ret_send.at[1 + s], ret_recv.at[1 + ranks[s]],
                   block_of(slot_z[s])).wait_send()


def body(embeds, doc_ids, prior_max, owned, owned_ids, owner_dest):
    n_grp, n_blk = lax.axis_size("grp"), lax.axis_size("blk")
    devices = n_grp * n_blk
    plan = make_plan(n_blk // 2)
    received, returns = plan[0], plan[5]
    slots = max(len(entry) for entry in received)
    rows, width = embeds.shape[1:]
    own_dev = owned.shape[0]
    vmem = pl.BlockSpec(memory_space=pltpu.VMEM)
    anywhere = pl.BlockSpec(memory_space=pl.ANY)
    dma = pltpu.SemaphoreType.DMA
    running, next_rows, next_ids = pl.pallas_call(
        functools.partial(kernel, plan, (n_grp, n_blk)),
        out_shape=(
            jax.ShapeDtypeStruct((1, rows), jnp.float32),
            jax.ShapeDtypeStruct((devices, CAP, width), jnp.bfloat16),
            jax.ShapeDtypeStruct((devices, 1, LANES), jnp.int32),
        ),
        in_specs=[anywhere, vmem, vmem, vmem, vmem, vmem],
        out_specs=(vmem, anywhere, anywhere),
        scratch_shapes=[
            pltpu.VMEM((2 + slots, rows, width), jnp.bfloat16),
            pltpu.VMEM((2 + slots, rows, width), jnp.bfloat16),
            pltpu.VMEM((2 + slots, 1, rows), jnp.int32),
            pltpu.VMEM((2 + slots, rows, LANES), jnp.float32),
            pltpu.VMEM((2 + slots, 1, rows), jnp.float32),
            pltpu.VMEM((1 + max(returns), 1, rows), jnp.float32),
            pltpu.VMEM((devices, CAP, width), jnp.bfloat16),
            pltpu.VMEM((devices, 1, LANES), jnp.int32),
            dma, dma((2 + slots, CHUNKS)), dma((2 + slots, CHUNKS)),
            dma((2 + slots,)), dma((2 + slots,)),
            dma((1 + slots,)), dma((1 + max(returns),)),
            dma, dma, dma, dma, dma((2,)),
        ],
        compiler_params=pltpu.CompilerParams(has_side_effects=True, vmem_limit_bytes=60 * 1024 * 1024),
    )(embeds, doc_ids, prior_max, owned, owned_ids.reshape(1, own_dev), owner_dest)
    return (running, next_rows.reshape(devices * CAP, width), next_ids[:, 0, :CAP].reshape(devices * CAP))


def solution(mesh):
    return jax.shard_map(
        body,
        mesh=mesh,
        in_specs=(
            P("grp", "blk", None),
            P("grp", "blk"),
            P("grp", "blk"),
            P(("grp", "blk"), None),
            P(("grp", "blk")),
            P(("grp", "blk"), None),
        ),
        out_specs=(P("grp", "blk"), P(("grp", "blk"), None), P(("grp", "blk"))),
        check_vma=False,
    )
```

profile of v0, /device:TPU:0, one launch (start us, length us, event | category | flops | bytes accessed | tf_op | source)
XLA Modules:
  0.0 95.4 jit_solution(1115419367403926545)
XLA Ops:
  0.6 1.4 %copy.10.dest = s32[64,1]{1,0:T(8,128)} copy(s32[64,1]{0,1:T(1,128)} %param.11) | data formatting | bytes 512 | tf_op args[5]
  2.0 89.0 %shard_map.85 = (f32[1,1024]{1,0:T(1,128)}, bf16[32,4,1024]{2,1,0:T(4,128)(2,1)}, s32[32,1,128]{2,1,0:T(1,128)}) custom-call(bf16[1,1024,1024]{2,1,0:T(8,128)(2,1)} %emb.1, s32[1,1024]{1,0:T(1,128)} %ids.1, f32[1,1024]{1,0:T(1,128)} %prior.1, bf16[64,1024]{1,0:T(8,128)(2,1)} %owned.1, s32[1,64]{1,0:T(1,128)} %bitcast.1, s32[64,1]{1,0:T(8,128)} %copy.10.dest), custom_call_target="tpu_custom_call" | custom-call | tf_op jit(solution)/shard_map/pallas_call | solution.py:352
  91.0 0.8 slice_reduce_fusion
  91.8 0.6 reshape_squeeze.3
  92.4 1.7 %reshape.13 = bf16[128,1024]{1,0:T(8,128)(2,1)} reshape(bf16[32,4,1024]{2,1,0:T(4,128)(2,1)} %get-tuple-element.7) | data formatting | bytes 524288 | tf_op jit(solution)/shard_map/reshape | solution.py:377
  94.1 1.3 %copy.12 = f32[1,1024]{1,0:T(1,128)} copy(f32[1,1024]{1,0:T(1,128)} %get-tuple-element.12) | data formatting | bytes 8192
where the time goes:
time: 95.7 us; the launch traced here: 95.4 us
  Pallas kernels  89 us (93%)
  local copies, waits for them, and re-layouts  5.73 us (6%)
    pallas_call x1, Pallas kernels, body(): pl.pallas_call(functools.partial(kernel, plan, (n_grp, n_blk)), out_shape...  89 us
    unnamed x2, local copies, waits for them, and re-layouts  2.64 us

commit v1 on v0

--- a/solution.py
+++ b/solution.py
@@ -15,12 +15,8 @@
 
 
 def make_plan(nz):
-    if nz == 4:
-        received = [[], [(0, 0)], [(1, 1), (0, 1), (3, 3)], [(1, 2), (0, 2)]]
-        late = [z == 3 for z in range(nz)]
-    else:
-        received = [[((z - 1) % nz, (z - 1) % nz), ((z - 2) % nz, (z - 1) % nz)] for z in range(nz)]
-        late = [False] * nz
+    received = [[((z - 1) % nz, (z - 1) % nz), ((z - 2) % nz, (z - 1) % nz)] for z in range(nz)]
+    late = [False] * nz
     own_to = [(-1, 0)] * nz
     forward = [[(-1, 0)] * len(received[z]) for z in range(nz)]
     rank = [[0] * len(received[z]) for z in range(nz)]
@@ -45,7 +41,7 @@
     return result
 
 
-def kernel(plan, sizes, emb, ids, prior, owned, owned_ids, dest,
+def ring_kernel(plan, sizes, emb, ids, prior, owned, owned_ids, dest,
            run_out, rows_out, ids_out,
            raw, nrm, idv, idt, acc, ret, obuf, oid,
            local_sem, send_sem, recv_sem, ids_send, ids_recv, ret_send, ret_recv,
@@ -149,7 +145,7 @@
     for k in range(CAP):
         here = jnp.where((dev_i == t_row) & (position == float(k)), number, 0.0)
         found = jnp.sum(here, axis=1, keepdims=True) - 1.0
-        outgoing_ids = jnp.where(lane_i == k, found, outgoing_ids)
+        outgoing_ids = jnp.where(lane_i % CAP == k, found, outgoing_ids)
     outgoing_ids = outgoing_ids.astype(jnp.int32)
     for d in range(devices):
         obuf[d] = outgoing[d * CAP:(d + 1) * CAP, :]
@@ -338,43 +334,461 @@
                    block_of(slot_z[s])).wait_send()
 
 
+OWN, PAIR, ONE, ZERO, THREE = range(5)
+SELF_UNIT = (OWN, OWN)
+OWN_PAIR = (PAIR, OWN)
+UNITS_FIRST = (
+    ((SELF_UNIT,), ()),
+    ((SELF_UNIT,), ()),
+    ((SELF_UNIT,), ((ONE, PAIR), OWN_PAIR)),
+    ((SELF_UNIT,), ((ONE, PAIR), OWN_PAIR)),
+)
+UNITS_SECOND = (
+    ((), (OWN_PAIR,)),
+    (((ZERO, OWN),), ((PAIR, ZERO), OWN_PAIR)),
+    (((ONE, OWN),), ((ZERO, PAIR), (THREE, OWN), (THREE, PAIR))),
+    ((), ((ZERO, OWN), (ZERO, PAIR))),
+)
+
+
+def line_kernel(sizes, emb, ids, prior, owned, owned_ids, dest,
+                run_out, rows_out, ids_out,
+                raw, nrm, idv, idt, acc, ret, obuf, oid, prior_v, owned_v, number_v, dest_v,
+                local_sem, in_sem, send_sem, recv_sem, ids_send, ids_recv, ret_send, ret_recv,
+                rows_send, rows_recv, oids_send, oids_recv, keep_sem):
+    n_grp, n_blk = sizes
+    devices = n_grp * n_blk
+    rows = emb.shape[1]
+    ch = rows // CHUNKS
+    half = ch // 2
+    g = lax.axis_index("grp")
+    b = lax.axis_index("blk")
+    flip = g % 2
+    z = b // 2
+    x = b % 2
+    role = z + flip * (3 - 2 * z)
+    partner = b + 1 - 2 * x
+    me = g * n_blk + b
+
+    def block_of(r):
+        return 2 * (r + flip * (3 - 2 * r)) + x
+
+    def to_device(step):
+        other = (me + step) % devices
+        return other, other // n_blk, other % n_blk
+
+    barrier = pltpu.get_barrier_semaphore()
+
+    @pl.loop(1, devices)
+    def _(step):
+        _, og, ob = to_device(step)
+        pl.semaphore_signal(barrier, inc=1, device_id=(og, ob), device_id_type=pl.DeviceIdType.MESH)
+
+    local = pltpu.make_async_copy(emb.at[0], raw.at[OWN], local_sem)
+    local.start()
+    inputs = [pltpu.make_async_copy(src, dst, in_sem.at[i]) for i, (src, dst) in enumerate((
+        (ids, idv.at[OWN]), (prior, prior_v), (owned, owned_v), (owned_ids, number_v), (dest, dest_v)))]
+    for copy in inputs:
+        copy.start()
+
+    pl.semaphore_wait(barrier, devices - 1)
+
+    def remote(src, dst, ssem, rsem, blk, grp=None):
+        return pltpu.make_async_remote_copy(
+            src_ref=src, dst_ref=dst, send_sem=ssem, recv_sem=rsem,
+            device_id=(g if grp is None else grp, blk), device_id_type=pl.DeviceIdType.MESH)
+
+    def piece(k):
+        if isinstance(k, int):
+            return pl.ds(k * half, half)
+        return pl.ds(pl.multiple_of(k * half, half), half)
+
+    def span(c):
+        return pl.ds(pl.multiple_of(c * ch, ch), ch)
+
+    whole = pl.ds(0, rows)
+    pieces = 2 * CHUNKS
+
+    own_slot = pick(role, [ZERO, ONE, ONE, THREE])
+    own_to = block_of(pick(role, [1, 2, 3, 2]))
+    has_own = role != 2
+    onward = block_of(role + 1)
+    gives_pair = (role > 0) | (x == 0)
+    takes_pair = (role > 0) | (x == 1)
+    early = role >= 2
+
+    def own_copy(k):
+        return remote(emb.at[0, piece(k), :], raw.at[own_slot, piece(k), :],
+                      send_sem.at[0, k], recv_sem.at[own_slot, k], own_to)
+
+    def pair_copy(k):
+        return remote(emb.at[0, piece(k), :], raw.at[PAIR, piece(k), :],
+                      send_sem.at[1, k], recv_sem.at[PAIR, k], partner)
+
+    def onward_copy(s, k):
+        return remote(raw.at[s, piece(k), :], raw.at[s, piece(k), :],
+                      send_sem.at[s, k], recv_sem.at[s, k], onward)
+
+    def ids_copy(src, lane, slot, blk):
+        return remote(src, idv.at[slot], ids_send.at[lane], ids_recv.at[slot], blk)
+
+    @pl.when(has_own)
+    def _():
+        ids_copy(ids, 0, own_slot, own_to).start()
+
+    @pl.when(role < 2)
+    def _():
+        for k in range(pieces):
+            own_copy(k).start()
+
+    @pl.when(gives_pair)
+    def _():
+        ids_copy(ids, 1, PAIR, partner).start()
+
+    def start_pair():
+        for k in range(pieces):
+            pair_copy(k).start()
+
+    @pl.when(early)
+    def _():
+        start_pair()
+
+    def normalize(values):
+        values = values.astype(jnp.float32)
+        scale = lax.rsqrt(jnp.sum(values * values, axis=-1, keepdims=True) + 1e-06)
+        return (values * scale).astype(jnp.bfloat16)
+
+    def ready(s, c):
+        at = span(c)
+        nrm[s, at, :] = normalize(raw[s, at, :])
+        for p in range(ch // LANES):
+            at = pl.ds(pl.multiple_of(c * ch + p * LANES, LANES), LANES)
+            line = idv[s, :, at].astype(jnp.float32)
+            idt[s, at, :] = jnp.transpose(jnp.broadcast_to(line, (LANES, LANES)))
+
+    def tile(row, row_at, width, col, col_at):
+        scores = lax.dot_general(
+            nrm[col, col_at, :], nrm[row, row_at, :], (((1,), (1,)), ((), ())),
+            preferred_element_type=jnp.float32)
+        row_ids = idv[row, :, row_at].astype(jnp.float32)
+        col_ids = idt[col, col_at, :]
+        parts = []
+        for p in range(width // LANES):
+            cut = slice(p * LANES, (p + 1) * LANES)
+            masked = jnp.where(col_ids < row_ids[:, cut], scores[:, cut], EMPTY)
+            parts.append(jnp.max(masked, axis=0, keepdims=True))
+        acc[row, :, row_at] = jnp.maximum(acc[row, :, row_at], jnp.concatenate(parts, axis=1))
+
+    for s in range(1, 5):
+        acc[s] = jnp.full((1, rows), EMPTY, jnp.float32)
+    for copy in inputs:
+        copy.wait()
+    acc[OWN] = prior_v[...]
+    local.wait()
+
+    @pl.loop(0, CHUNKS)
+    def _(c):
+        ready(OWN, c)
+
+    own_dev = owned.shape[0]
+    owned_normed = normalize(owned_v[...])
+    t_col = dest_v[...].reshape(own_dev, 1).astype(jnp.float32)
+    t_row = jnp.transpose(jnp.broadcast_to(t_col, (own_dev, LANES)))[0:1, :]
+    row_i = lax.broadcasted_iota(jnp.int32, (own_dev, own_dev), 0)
+    col_i = lax.broadcasted_iota(jnp.int32, (own_dev, own_dev), 1)
+    earlier = jnp.where((row_i < col_i) & (t_col == t_row), 1.0, 0.0)
+    position = jnp.sum(earlier, axis=0, keepdims=True)
+    place = t_row * CAP + position
+    which = lax.broadcasted_iota(jnp.int32, (devices * CAP, own_dev), 0).astype(jnp.float32)
+    onehot = jnp.where(which == place, 1.0, 0.0).astype(jnp.bfloat16)
+    outgoing = jnp.dot(onehot, owned_normed, preferred_element_type=jnp.float32).astype(jnp.bfloat16)
+    dev_i = lax.broadcasted_iota(jnp.int32, (devices, own_dev), 0).astype(jnp.float32)
+    lane_i = lax.broadcasted_iota(jnp.int32, (devices, LANES), 1)
+    number = number_v[...].astype(jnp.float32) + 1.0
+    outgoing_ids = jnp.full((devices, LANES), -1.0, jnp.float32)
+    for k in range(CAP):
+        here = jnp.where((dev_i == t_row) & (position == float(k)), number, 0.0)
+        found = jnp.sum(here, axis=1, keepdims=True) - 1.0
+        outgoing_ids = jnp.where(lane_i % CAP == k, found, outgoing_ids)
+    outgoing_ids = outgoing_ids.astype(jnp.int32)
+    for d in range(devices):
+        obuf[d] = outgoing[d * CAP:(d + 1) * CAP, :]
+        oid[d] = outgoing_ids[d:d + 1, :]
+
+    keep_rows = pltpu.make_async_copy(obuf.at[me], rows_out.at[me], keep_sem.at[0])
+    keep_ids = pltpu.make_async_copy(oid.at[me], ids_out.at[me], keep_sem.at[1])
+
+    def start_routing():
+        @pl.loop(1, devices)
+        def _(step):
+            other, og, ob = to_device(step)
+            remote(obuf.at[other], rows_out.at[me], rows_send, rows_recv, ob, og).start()
+            remote(oid.at[other], ids_out.at[me], oids_send, oids_recv, ob, og).start()
+
+        keep_rows.start()
+        keep_ids.start()
+
+    def is_row(u, v):
+        diff = (u - v + n_blk) % n_blk
+        return (diff >= 1) & (diff <= CYCLE)
+
+    slot_blocks = [b, partner, block_of(1), block_of(0), block_of(3)]
+
+    def block_in(slot):
+        result = slot_blocks[0]
+        for i in range(1, 5):
+            result = jnp.where(slot == i, slot_blocks[i], result)
+        return result
+
+    def run_units(table, phase, c):
+        longest = max(len(entry) for by_phase in table for entry in by_phase)
+        lists = [entry for by_phase in table for entry in by_phase]
+        which_list = role * 2 + phase
+        ends = [int(len(entry) > 0 and entry[-1] == OWN_PAIR) for entry in lists]
+        count = pick(which_list, [len(entry) for entry in lists]) - pick(which_list, ends) * (1 - x)
+
+        @pl.loop(0, count)
+        def _(j):
+            def entry(i):
+                return pick(j * len(lists) + which_list,
+                            [(lst[n] if n < len(lst) else (0, 0))[i] for n in range(longest) for lst in lists])
+
+            u, v = entry(0), entry(1)
+            bu, bv = block_in(u), block_in(v)
+
+            @pl.when(is_row(bv, bu) | (u == v))
+            def _():
+                tile(v, whole, rows, u, span(c))
+
+            @pl.when(is_row(bu, bv))
+            def _():
+                tile(u, span(c), ch, v, whole)
+
+    def ids_wait(s):
+        ids_copy(idv.at[s], 1, s, partner).wait_recv()
+
+    def stream_wait(s, k):
+        remote(raw.at[s, piece(k), :], raw.at[s, piece(k), :], send_sem.at[1, k], recv_sem.at[s, k], partner).wait_recv()
+
+    routing_step = pick(role, [CHUNKS - 1, CHUNKS - 1, 2 * CHUNKS - 1, 2 * CHUNKS - 1])
+
+    @pl.loop(0, 2 * CHUNKS)
+    def _(p):
+        phase = p // CHUNKS
+        c = p % CHUNKS
+        has_in = role > phase
+        s_in = jnp.where((phase == 1) | (role == 1), ZERO, ONE)
+
+        def take(k, first):
+            @pl.when(has_in)
+            def _():
+                stream_wait(s_in, k)
+                if first:
+                    @pl.when(c == 0)
+                    def _():
+                        ids_wait(s_in)
+
+                @pl.when(role < 3)
+                def _():
+                    onward_copy(s_in, k).start()
+                    if first:
+                        @pl.when(c == 0)
+                        def _():
+                            ids_copy(idv.at[s_in], s_in, s_in, onward).start()
+
+            @pl.when((phase == 0) & (role == 3))
+            def _():
+                own_copy(k).start()
+
+            @pl.when((phase == 0) & (role == 0))
+            def _():
+                own_copy(k).wait_send()
+
+        take(2 * c, True)
+
+        @pl.when((p == 2) & (role < 2) & gives_pair)
+        def _():
+            start_pair()
+
+        run_units(UNITS_FIRST, phase, c)
+        take(2 * c + 1, False)
+
+        @pl.when(p == routing_step)
+        def _():
+            start_routing()
+
+        @pl.when(has_in)
+        def _():
+            ready(s_in, c)
+
+        @pl.when((early == (phase == 0)) & takes_pair)
+        def _():
+            @pl.when(c == 0)
+            def _():
+                ids_wait(PAIR)
+
+            stream_wait(PAIR, 2 * c)
+            stream_wait(PAIR, 2 * c + 1)
+            ready(PAIR, c)
+
+        @pl.when((role == 2) & (phase == 1))
+        def _():
+            @pl.when(c == 0)
+            def _():
+                ids_wait(THREE)
+
+            stream_wait(THREE, 2 * c)
+            stream_wait(THREE, 2 * c + 1)
+            ready(THREE, c)
+
+        run_units(UNITS_SECOND, phase, c)
+
+    def back(slot, index, r):
+        return remote(acc.at[slot], ret.at[index], ret_send.at[slot], ret_recv.at[index],
+                      partner if r is None else block_of(r))
+
+    returns = [(role > 0, PAIR, 0, None), (role == 1, ZERO, 1, 0), (role == 2, ZERO, 2, 0), (role == 3, ZERO, 3, 0),
+               (role == 2, ONE, 2, 1), (role == 3, ONE, 3, 1), (role == 2, THREE, 2, 3)]
+    for when, slot, index, r in reversed(returns):
+        @pl.when(when)
+        def _(slot=slot, index=index, r=r):
+            back(slot, index, r).start()
+
+    @pl.when(gives_pair)
+    def _():
+        ids_copy(ids, 1, PAIR, partner).wait_send()
+        for k in range(pieces):
+            pair_copy(k).wait_send()
+
+    @pl.when(has_own)
+    def _():
+        ids_copy(ids, 0, own_slot, own_to).wait_send()
+
+    @pl.when((role == 1) | (role == 3))
+    def _():
+        for k in range(pieces):
+            own_copy(k).wait_send()
+
+    for s, sends in ((ONE, role == 2), (ZERO, (role == 1) | (role == 2))):
+        @pl.when(sends)
+        def _(s=s):
+            ids_copy(idv.at[s], s, s, onward).wait_send()
+            for k in range(pieces):
+                onward_copy(s, k).wait_send()
+
+    keep_rows.wait()
+    keep_ids.wait()
+    others = pl.ds(0, devices - 1)
+    pltpu.make_async_copy(obuf.at[others], rows_out.at[others], rows_send).wait()
+    pltpu.make_async_copy(oid.at[others], ids_out.at[others], oids_send).wait()
+    pltpu.make_async_copy(obuf.at[others], rows_out.at[others], rows_recv).wait()
+    pltpu.make_async_copy(oid.at[others], ids_out.at[others], oids_recv).wait()
+
+    run_out[...] = acc[OWN]
+    for index, gets in enumerate((role > 0, role == 0, (role != 2), role < 2)):
+        @pl.when(gets)
+        def _(index=index):
+            remote(acc.at[PAIR], ret.at[index], ret_send.at[PAIR], ret_recv.at[index], partner).wait_recv()
+            run_out[...] = jnp.maximum(run_out[...], ret[index])
+
+    for when, slot, index, r in returns:
+        @pl.when(when)
+        def _(slot=slot, index=index, r=r):
+            back(slot, index, r).wait_send()
+
+
+def place_kernel(run, routed, routed_ids, run_out, rows_out, ids_out):
+    run_out[...] = run[...]
+    devices, cap, _ = routed.shape
+    for d in range(0, devices, 2):
+        both = jnp.concatenate([routed[d].astype(jnp.float32), routed[d + 1].astype(jnp.float32)], axis=0)
+        rows_out[d * cap:(d + 2) * cap, :] = both.astype(jnp.bfloat16)
+    lines = routed_ids[...].reshape(devices, LANES)
+    for part in range(devices * cap // LANES):
+        sub = lines[part * LANES // cap:(part + 1) * LANES // cap, :]
+        row_i = lax.broadcasted_iota(jnp.int32, sub.shape, 0)
+        lane_i = lax.broadcasted_iota(jnp.int32, sub.shape, 1)
+        mine = jnp.where(lane_i // cap == row_i, sub, 0)
+        ids_out[:, part * LANES:(part + 1) * LANES] = jnp.sum(mine, axis=0, keepdims=True)
+
+
 def body(embeds, doc_ids, prior_max, owned, owned_ids, owner_dest):
     n_grp, n_blk = lax.axis_size("grp"), lax.axis_size("blk")
     devices = n_grp * n_blk
-    plan = make_plan(n_blk // 2)
-    received, returns = plan[0], plan[5]
-    slots = max(len(entry) for entry in received)
+    line = n_blk == 8
     rows, width = embeds.shape[1:]
     own_dev = owned.shape[0]
     vmem = pl.BlockSpec(memory_space=pltpu.VMEM)
     anywhere = pl.BlockSpec(memory_space=pl.ANY)
     dma = pltpu.SemaphoreType.DMA
+    shapes = (
+        jax.ShapeDtypeStruct((1, rows), jnp.float32),
+        jax.ShapeDtypeStruct((devices, CAP, width), jnp.bfloat16),
+        jax.ShapeDtypeStruct((devices, 1, LANES), jnp.int32),
+    )
+    limit = 60 * 1024 * 1024
+    if line:
+        slots, pieces = 5, 2 * CHUNKS
+        results = pl.pallas_call(
+            functools.partial(line_kernel, (n_grp, n_blk)),
+            out_shape=shapes,
+            in_specs=[anywhere] * 6,
+            out_specs=(vmem, anywhere, anywhere),
+            scratch_shapes=[
+                pltpu.VMEM((slots, rows, width), jnp.bfloat16),
+                pltpu.VMEM((slots, rows, width), jnp.bfloat16),
+                pltpu.VMEM((slots, 1, rows), jnp.int32),
+                pltpu.VMEM((slots, rows, LANES), jnp.float32),
+                pltpu.VMEM((slots, 1, rows), jnp.float32),
+                pltpu.VMEM((4, 1, rows), jnp.float32),
+                pltpu.VMEM((devices, CAP, width), jnp.bfloat16),
+                pltpu.VMEM((devices, 1, LANES), jnp.int32),
+                pltpu.VMEM((1, rows), jnp.float32),
+                pltpu.VMEM((own_dev, width), jnp.bfloat16),
+                pltpu.VMEM((1, own_dev), jnp.int32),
+                pltpu.VMEM((own_dev, 1, 1), jnp.int32),
+                dma, dma((5,)), dma((slots, pieces)), dma((slots, pieces)),
+                dma((slots,)), dma((slots,)), dma((slots,)), dma((4,)),
+                dma, dma, dma, dma, dma((2,)),
+            ],
+            compiler_params=pltpu.CompilerParams(has_side_effects=True, collective_id=0, vmem_limit_bytes=limit),
+        )(embeds, doc_ids, prior_max, owned, owned_ids.reshape(1, own_dev), owner_dest.reshape(own_dev, 1, 1))
+    else:
+        plan = make_plan(n_blk // 2)
+        received, returns = plan[0], plan[5]
+        slots = max(len(entry) for entry in received)
+        results = pl.pallas_call(
+            functools.partial(ring_kernel, plan, (n_grp, n_blk)),
+            out_shape=shapes,
+            in_specs=[anywhere, vmem, vmem, vmem, vmem, vmem],
+            out_specs=(vmem, anywhere, anywhere),
+            scratch_shapes=[
+                pltpu.VMEM((2 + slots, rows, width), jnp.bfloat16),
+                pltpu.VMEM((2 + slots, rows, width), jnp.bfloat16),
+                pltpu.VMEM((2 + slots, 1, rows), jnp.int32),
+                pltpu.VMEM((2 + slots, rows, LANES), jnp.float32),
+                pltpu.VMEM((2 + slots, 1, rows), jnp.float32),
+                pltpu.VMEM((1 + max(returns), 1, rows), jnp.float32),
+                pltpu.VMEM((devices, CAP, width), jnp.bfloat16),
+                pltpu.VMEM((devices, 1, LANES), jnp.int32),
+                dma, dma((2 + slots, CHUNKS)), dma((2 + slots, CHUNKS)),
+                dma((2 + slots,)), dma((2 + slots,)),
+                dma((1 + slots,)), dma((1 + max(returns),)),
+                dma, dma, dma, dma, dma((2,)),
+            ],
+            compiler_params=pltpu.CompilerParams(has_side_effects=True, vmem_limit_bytes=limit),
+        )(embeds, doc_ids, prior_max, owned, owned_ids.reshape(1, own_dev), owner_dest)
     running, next_rows, next_ids = pl.pallas_call(
-        functools.partial(kernel, plan, (n_grp, n_blk)),
+        place_kernel,
         out_shape=(
             jax.ShapeDtypeStruct((1, rows), jnp.float32),
-            jax.ShapeDtypeStruct((devices, CAP, width), jnp.bfloat16),
-            jax.ShapeDtypeStruct((devices, 1, LANES), jnp.int32),
+            jax.ShapeDtypeStruct((devices * CAP, width), jnp.bfloat16),
+            jax.ShapeDtypeStruct((1, devices * CAP), jnp.int32),
         ),
-        in_specs=[anywhere, vmem, vmem, vmem, vmem, vmem],
-        out_specs=(vmem, anywhere, anywhere),
-        scratch_shapes=[
-            pltpu.VMEM((2 + slots, rows, width), jnp.bfloat16),
-            pltpu.VMEM((2 + slots, rows, width), jnp.bfloat16),
-            pltpu.VMEM((2 + slots, 1, rows), jnp.int32),
-            pltpu.VMEM((2 + slots, rows, LANES), jnp.float32),
-            pltpu.VMEM((2 + slots, 1, rows), jnp.float32),
-            pltpu.VMEM((1 + max(returns), 1, rows), jnp.float32),
-            pltpu.VMEM((devices, CAP, width), jnp.bfloat16),
-            pltpu.VMEM((devices, 1, LANES), jnp.int32),
-            dma, dma((2 + slots, CHUNKS)), dma((2 + slots, CHUNKS)),
-            dma((2 + slots,)), dma((2 + slots,)),
-            dma((1 + slots,)), dma((1 + max(returns),)),
-            dma, dma, dma, dma, dma((2,)),
-        ],
-        compiler_params=pltpu.CompilerParams(has_side_effects=True, vmem_limit_bytes=60 * 1024 * 1024),
-    )(embeds, doc_ids, prior_max, owned, owned_ids.reshape(1, own_dev), owner_dest)
-    return (running, next_rows.reshape(devices * CAP, width), next_ids[:, 0, :CAP].reshape(devices * CAP))
+        in_specs=[vmem] * 3,
+        out_specs=(vmem,) * 3,
+    )(*results)
+    return (running, next_rows, next_ids.reshape(devices * CAP))
 
 
 def solution(mesh):

time: 95.7 us -> 77.8 us (0.81)
  Pallas kernels: 89 us -> 75.6 us
  local copies, waits for them, and re-layouts: 5.73 us -> 1.36 us
    pallas_call x1 -> x2, Pallas kernels: 89 us -> 75.6 us  [the longest x1 73.9 us: body(): pl.pallas_call(functools.partial(line_kernel, (n_grp, n_blk)), out_shape=...]
    unnamed x2 -> x0, local copies, waits for them, and re-layouts: 2.64 us -> none
where the time goes in v1:
time: 77.8 us; the launch traced here: 77.6 us
  Pallas kernels  75.6 us (97%)
  local copies, waits for them, and re-layouts  1.36 us (2%)
    pallas_call x1, Pallas kernels, body(): pl.pallas_call(functools.partial(line_kernel, (n_grp, n_blk)), out_shape=...  73.9 us
    pallas_call x1, Pallas kernels, body(): pl.pallas_call(place_kernel, out_shape=(jax.ShapeDtypeStruct((1, rows), j...  1.72 us

profile of v1, /device:TPU:0, one launch (start us, length us, event | category | flops | bytes accessed | tf_op | source)
XLA Modules:
  0.0 77.6 jit_solution(2412925077306104032)
XLA Ops:
  0.6 1.4 %copy.9.dest = s32[64,1,1]{2,1,0:T(1,128)} copy(s32[64,1,1]{0,2,1:T(1,128)} %bitcast.3) | data formatting | bytes 512 | tf_op jit(solution)/shard_map/reshape | solution.py:755
  2.0 73.9 %shard_map.85 = (f32[1,1024]{1,0:T(1,128)}, bf16[32,4,1024]{2,1,0:T(4,128)(2,1)}, s32[32,1,128]{2,1,0:T(1,128)}) custom-call(bf16[1,1024,1024]{2,1,0:T(8,128)(2,1)} %emb.1, s32[1,1024]{1,0:T(1,128)} %ids.1, f32[1,1024]{1,0:T(1,128)} %prior.1, bf16[64,1024]{1,0:T(8,128)(2,1)} %owned.1, s32[1,64]{1,0:T(1,128)} %bitcast.4, s32[64,1,1]{2,1,0:T(1,128)} %copy.9.dest), custom_call_target="tpu_custom_call" | custom-call | tf_op jit(solution)/shard_map/pallas_call | solution.py:732
  75.9 1.7 %shard_map.86 = (f32[1,1024]{1,0:T(1,128)}, bf16[128,1024]{1,0:T(8,128)(2,1)}, s32[1,128]{1,0:T(1,128)}) custom-call(f32[1,1024]{1,0:T(1,128)} %get-tuple-element.9.run, bf16[32,4,1024]{2,1,0:T(4,128)(2,1)} %get-tuple-element.10.routed, s32[32,1,128]{2,1,0:T(1,128)} %get-tuple-element.11.routed_ids), custom_call_target="tpu_custom_call" | custom-call | tf_op jit(solution)/shard_map/pallas_call | solution.py:781

commit v2 on v1

--- a/solution.py
+++ b/solution.py
@@ -334,6 +334,10 @@
                    block_of(slot_z[s])).wait_send()
 
 
+SPLIT = 4
+LEAD = 4
+LATE_LEAD = 4
+LATE_STEP = 3
 OWN, PAIR, ONE, ZERO, THREE = range(5)
 SELF_UNIT = (OWN, OWN)
 OWN_PAIR = (PAIR, OWN)
@@ -355,12 +359,12 @@
                 run_out, rows_out, ids_out,
                 raw, nrm, idv, idt, acc, ret, obuf, oid, prior_v, owned_v, number_v, dest_v,
                 local_sem, in_sem, send_sem, recv_sem, ids_send, ids_recv, ret_send, ret_recv,
-                rows_send, rows_recv, oids_send, oids_recv, keep_sem):
+                rows_send, rows_recv, oids_send, oids_recv, keep_sem, known_sem):
     n_grp, n_blk = sizes
     devices = n_grp * n_blk
     rows = emb.shape[1]
     ch = rows // CHUNKS
-    half = ch // 2
+    part = ch // SPLIT
     g = lax.axis_index("grp")
     b = lax.axis_index("blk")
     flip = g % 2
@@ -379,10 +383,22 @@
 
     barrier = pltpu.get_barrier_semaphore()
 
-    @pl.loop(1, devices)
-    def _(step):
-        _, og, ob = to_device(step)
-        pl.semaphore_signal(barrier, inc=1, device_id=(og, ob), device_id_type=pl.DeviceIdType.MESH)
+    def signal(semaphore, grp, blk):
+        pl.semaphore_signal(semaphore, inc=1, device_id=(grp, blk), device_id_type=pl.DeviceIdType.MESH)
+
+    other_core = g + 1 - 2 * flip
+    other_row = (g + n_grp // 2) % n_grp
+    signal(barrier, g, partner)
+    signal(barrier, other_core, b)
+    signal(barrier, other_row, b)
+
+    @pl.when(z > 0)
+    def _():
+        signal(barrier, g, b - 2)
+
+    @pl.when(z < 3)
+    def _():
+        signal(barrier, g, b + 2)
 
     local = pltpu.make_async_copy(emb.at[0], raw.at[OWN], local_sem)
     local.start()
@@ -391,7 +407,18 @@
     for copy in inputs:
         copy.start()
 
-    pl.semaphore_wait(barrier, devices - 1)
+    pl.semaphore_wait(barrier, jnp.where((z == 1) | (z == 2), 5, 4))
+
+    def told(here, index, then=None):
+        @pl.when(here)
+        def _():
+            if index is not None:
+                pl.semaphore_wait(known_sem.at[index], 1)
+            if then is not None:
+                signal(known_sem.at[then[0]], then[1], then[2])
+
+    told(z == 0, None, (0, g, b + 2))
+    told(z == 3, None, (1, g, b - 2))
 
     def remote(src, dst, ssem, rsem, blk, grp=None):
         return pltpu.make_async_remote_copy(
@@ -400,14 +427,14 @@
 
     def piece(k):
         if isinstance(k, int):
-            return pl.ds(k * half, half)
-        return pl.ds(pl.multiple_of(k * half, half), half)
+            return pl.ds(k * part, part)
+        return pl.ds(pl.multiple_of(k * part, part), part)
 
     def span(c):
         return pl.ds(pl.multiple_of(c * ch, ch), ch)
 
     whole = pl.ds(0, rows)
-    pieces = 2 * CHUNKS
+    pieces = SPLIT * CHUNKS
 
     own_slot = pick(role, [ZERO, ONE, ONE, THREE])
     own_to = block_of(pick(role, [1, 2, 3, 2]))
@@ -445,13 +472,10 @@
     def _():
         ids_copy(ids, 1, PAIR, partner).start()
 
-    def start_pair():
-        for k in range(pieces):
+    @pl.when(early)
+    def _():
+        for k in range(LEAD):
             pair_copy(k).start()
-
-    @pl.when(early)
-    def _():
-        start_pair()
 
     def normalize(values):
         values = values.astype(jnp.float32)
@@ -490,10 +514,13 @@
     def _(c):
         ready(OWN, c)
 
+    told(z == 1, 0, (0, g, b + 2))
+    told(z == 2, 1, (1, g, b - 2))
+
     own_dev = owned.shape[0]
     owned_normed = normalize(owned_v[...])
-    t_col = dest_v[...].reshape(own_dev, 1).astype(jnp.float32)
-    t_row = jnp.transpose(jnp.broadcast_to(t_col, (own_dev, LANES)))[0:1, :]
+    t_row = dest_v[...].astype(jnp.float32)
+    t_col = jnp.transpose(jnp.broadcast_to(t_row, (LANES, own_dev)))[:, 0:1]
     row_i = lax.broadcasted_iota(jnp.int32, (own_dev, own_dev), 0)
     col_i = lax.broadcasted_iota(jnp.int32, (own_dev, own_dev), 1)
     earlier = jnp.where((row_i < col_i) & (t_col == t_row), 1.0, 0.0)
@@ -515,6 +542,9 @@
         obuf[d] = outgoing[d * CAP:(d + 1) * CAP, :]
         oid[d] = outgoing_ids[d:d + 1, :]
 
+    told(z == 2, 0, (0, g, b + 2))
+    told(z == 1, 1, (1, g, b - 2))
+
     keep_rows = pltpu.make_async_copy(obuf.at[me], rows_out.at[me], keep_sem.at[0])
     keep_ids = pltpu.make_async_copy(oid.at[me], ids_out.at[me], keep_sem.at[1])
 
@@ -570,8 +600,6 @@
     def stream_wait(s, k):
         remote(raw.at[s, piece(k), :], raw.at[s, piece(k), :], send_sem.at[1, k], recv_sem.at[s, k], partner).wait_recv()
 
-    routing_step = pick(role, [CHUNKS - 1, CHUNKS - 1, 2 * CHUNKS - 1, 2 * CHUNKS - 1])
-
     @pl.loop(0, 2 * CHUNKS)
     def _(p):
         phase = p // CHUNKS
@@ -579,11 +607,13 @@
         has_in = role > phase
         s_in = jnp.where((phase == 1) | (role == 1), ZERO, ONE)
 
-        def take(k, first):
+        def take(i):
+            k = SPLIT * c + i
+
             @pl.when(has_in)
             def _():
                 stream_wait(s_in, k)
-                if first:
+                if i == 0:
                     @pl.when(c == 0)
                     def _():
                         ids_wait(s_in)
@@ -591,54 +621,92 @@
                 @pl.when(role < 3)
                 def _():
                     onward_copy(s_in, k).start()
-                    if first:
+                    if i == 0:
                         @pl.when(c == 0)
                         def _():
                             ids_copy(idv.at[s_in], s_in, s_in, onward).start()
 
-            @pl.when((phase == 0) & (role == 3))
-            def _():
-                own_copy(k).start()
-
             @pl.when((phase == 0) & (role == 0))
             def _():
                 own_copy(k).wait_send()
 
-        take(2 * c, True)
-
-        @pl.when((p == 2) & (role < 2) & gives_pair)
-        def _():
-            start_pair()
+            @pl.when((phase == 0) & early & (k + LEAD < pieces))
+            def _():
+                pair_copy(k + LEAD).start()
+
+            @pl.when((phase == 0) & (role == 3) & (k >= pieces // 2))
+            def _():
+                own_copy(2 * k - pieces).start()
+                own_copy(2 * k - pieces + 1).start()
+
+            if i == 0:
+                @pl.when((phase == 1) & (role < 2) & takes_pair & (c == 0))
+                def _():
+                    ids_wait(PAIR)
+
+            @pl.when((phase == 1) & (role < 2) & takes_pair)
+            def _():
+                stream_wait(PAIR, k)
+
+            @pl.when((phase == 1) & (role == 0) & gives_pair)
+            def _():
+                pair_copy(k).wait_send()
+
+            @pl.when((phase == 1) & (role < 2) & gives_pair & (k + LATE_LEAD < pieces))
+            def _():
+                pair_copy(k + LATE_LEAD).start()
+
+        for i in range(SPLIT // 2):
+            take(i)
+
+        @pl.when((p == LATE_STEP) & (role < 2) & gives_pair)
+        def _():
+            for k in range(LATE_LEAD):
+                pair_copy(k).start()
+
+        @pl.when((p == 2 * CHUNKS - 1) & (role != 2))
+        def _():
+            start_routing()
 
         run_units(UNITS_FIRST, phase, c)
-        take(2 * c + 1, False)
-
-        @pl.when(p == routing_step)
+        for i in range(SPLIT // 2, SPLIT):
+            take(i)
+
+        @pl.when((p == 2 * CHUNKS - 1) & (role == 2))
         def _():
             start_routing()
 
+        told((p == 0) & (z == 3), 0)
+        told((p == 0) & (z == 0), 1)
+        told(p == 0, None, (2, other_core, b))
+        told(p == 1, 2, (3, other_row, b))
+        told(p == 2, 3)
+
         @pl.when(has_in)
         def _():
             ready(s_in, c)
 
+        @pl.when((phase == 0) & early)
+        def _():
+            @pl.when(c == 0)
+            def _():
+                ids_wait(PAIR)
+
+            for i in range(SPLIT):
+                stream_wait(PAIR, SPLIT * c + i)
+
         @pl.when((early == (phase == 0)) & takes_pair)
         def _():
+            ready(PAIR, c)
+
+        @pl.when((role == 2) & (phase == 1))
+        def _():
             @pl.when(c == 0)
             def _():
-                ids_wait(PAIR)
-
-            stream_wait(PAIR, 2 * c)
-            stream_wait(PAIR, 2 * c + 1)
-            ready(PAIR, c)
-
-        @pl.when((role == 2) & (phase == 1))
-        def _():
-            @pl.when(c == 0)
-            def _():
                 ids_wait(THREE)
 
-            stream_wait(THREE, 2 * c)
-            stream_wait(THREE, 2 * c + 1)
+            for i in range(SPLIT):
+                stream_wait(THREE, SPLIT * c + i)
             ready(THREE, c)
 
         run_units(UNITS_SECOND, phase, c)
@@ -657,6 +725,9 @@
     @pl.when(gives_pair)
     def _():
         ids_copy(ids, 1, PAIR, partner).wait_send()
+
+    @pl.when(role > 0)
+    def _():
         for k in range(pieces):
             pair_copy(k).wait_send()
 
@@ -715,7 +786,7 @@
 def body(embeds, doc_ids, prior_max, owned, owned_ids, owner_dest):
     n_grp, n_blk = lax.axis_size("grp"), lax.axis_size("blk")
     devices = n_grp * n_blk
-    line = n_blk == 8
+    line = (n_grp, n_blk) == (4, 8)
     rows, width = embeds.shape[1:]
     own_dev = owned.shape[0]
     vmem = pl.BlockSpec(memory_space=pltpu.VMEM)
@@ -728,7 +799,7 @@
     )
     limit = 60 * 1024 * 1024
     if line:
-        slots, pieces = 5, 2 * CHUNKS
+        slots, pieces = 5, SPLIT * CHUNKS
         results = pl.pallas_call(
             functools.partial(line_kernel, (n_grp, n_blk)),
             out_shape=shapes,
@@ -746,13 +817,13 @@
                 pltpu.VMEM((1, rows), jnp.float32),
                 pltpu.VMEM((own_dev, width), jnp.bfloat16),
                 pltpu.VMEM((1, own_dev), jnp.int32),
-                pltpu.VMEM((own_dev, 1, 1), jnp.int32),
+                pltpu.VMEM((1, own_dev), jnp.int32),
                 dma, dma((5,)), dma((slots, pieces)), dma((slots, pieces)),
                 dma((slots,)), dma((slots,)), dma((slots,)), dma((4,)),
-                dma, dma, dma, dma, dma((2,)),
+                dma, dma, dma, dma, dma((2,)), pltpu.SemaphoreType.REGULAR((4,)),
             ],
             compiler_params=pltpu.CompilerParams(has_side_effects=True, collective_id=0, vmem_limit_bytes=limit),
-        )(embeds, doc_ids, prior_max, owned, owned_ids.reshape(1, own_dev), owner_dest.reshape(own_dev, 1, 1))
+        )(embeds, doc_ids, prior_max, owned, owned_ids.reshape(1, own_dev), owner_dest.reshape(1, own_dev))
     else:
         plan = make_plan(n_blk // 2)
         received, returns = plan[0], plan[5]

time: 77.8 us -> 71.2 us (0.915)
  Pallas kernels: 75.6 us -> 70.4 us
  local copies, waits for them, and re-layouts: 1.36 us -> 0 us
    pallas_call x1, Pallas kernels: 73.9 us -> 68.7 us  [body(): pl.pallas_call(functools.partial(line_kernel, (n_grp, n_blk)), out_shape=...]
    reshape x1 -> x0, local copies, waits for them, and re-layouts: 1.36 us -> none  [body(): owner_dest.reshape(own_dev, 1, 1)]
where the time goes in v2:
time: 71.2 us; the launch traced here: 71 us
  Pallas kernels  70.4 us (99%)
    pallas_call x1, Pallas kernels, body(): pl.pallas_call(functools.partial(line_kernel, (n_grp, n_blk)), out_shape=...  68.7 us
    pallas_call x1, Pallas kernels, body(): pl.pallas_call(place_kernel, out_shape=(jax.ShapeDtypeStruct((1, rows), j...  1.72 us

profile of v2, /device:TPU:0, one launch (start us, length us, event | category | flops | bytes accessed | tf_op | source)
XLA Modules:
  0.0 71.0 jit_solution(2677374997732871642)
XLA Ops:
  0.6 68.7 %shard_map.85 = (f32[1,1024]{1,0:T(1,128)}, bf16[32,4,1024]{2,1,0:T(4,128)(2,1)}, s32[32,1,128]{2,1,0:T(1,128)}) custom-call(bf16[1,1024,1024]{2,1,0:T(8,128)(2,1)} %emb.1, s32[1,1024]{1,0:T(1,128)} %ids.1, f32[1,1024]{1,0:T(1,128)} %prior.1, bf16[64,1024]{1,0:T(8,128)(2,1)} %owned.1, s32[1,64]{1,0:T(1,128)} %bitcast.3, s32[1,64]{1,0:T(1,128)} %bitcast.4), custom_call_target="tpu_custom_call" | custom-call | tf_op jit(solution)/shard_map/pallas_call | solution.py:803
  69.3 1.7 %shard_map.86 = (f32[1,1024]{1,0:T(1,128)}, bf16[128,1024]{1,0:T(8,128)(2,1)}, s32[1,128]{1,0:T(1,128)}) custom-call(f32[1,1024]{1,0:T(1,128)} %get-tuple-element.9.run, bf16[32,4,1024]{2,1,0:T(4,128)(2,1)} %get-tuple-element.10.routed, s32[32,1,128]{2,1,0:T(1,128)} %get-tuple-element.11.routed_ids), custom_call_target="tpu_custom_call" | custom-call | tf_op jit(solution)/shard_map/pallas_call | solution.py:852

commit v3 on v2

--- a/solution.py
+++ b/solution.py
@@ -335,30 +335,25 @@
 
 
 SPLIT = 4
-LEAD = 4
-LATE_LEAD = 4
+LATE_LEAD = 2
 LATE_STEP = 3
+THREE_FROM = 7
 OWN, PAIR, ONE, ZERO, THREE = range(5)
 SELF_UNIT = (OWN, OWN)
 OWN_PAIR = (PAIR, OWN)
-UNITS_FIRST = (
-    ((SELF_UNIT,), ()),
-    ((SELF_UNIT,), ()),
-    ((SELF_UNIT,), ((ONE, PAIR), OWN_PAIR)),
-    ((SELF_UNIT,), ((ONE, PAIR), OWN_PAIR)),
+UNITS = (
+    (((), ()), ((), ()), ((), ((THREE, OWN),)), ((), ())),
+    (((SELF_UNIT,), ()), ((SELF_UNIT,), ()), ((SELF_UNIT,), ((ZERO, PAIR),)), ((SELF_UNIT,), ((ZERO, PAIR),))),
+    (((), ()), ((), ()), ((), ((THREE, PAIR),)), ((), ())),
+    (((), (OWN_PAIR,)), (((ZERO, OWN),), ((PAIR, ZERO), OWN_PAIR)),
+     ((OWN_PAIR,), ((ONE, OWN), (ONE, PAIR))), (((ZERO, OWN), OWN_PAIR), ((ONE, PAIR),))),
 )
-UNITS_SECOND = (
-    ((), (OWN_PAIR,)),
-    (((ZERO, OWN),), ((PAIR, ZERO), OWN_PAIR)),
-    (((ONE, OWN),), ((ZERO, PAIR), (THREE, OWN), (THREE, PAIR))),
-    ((), ((ZERO, OWN), (ZERO, PAIR))),
-)
 
 
 def line_kernel(sizes, emb, ids, prior, owned, owned_ids, dest,
-                run_out, rows_out, ids_out,
-                raw, nrm, idv, idt, acc, ret, obuf, oid, prior_v, owned_v, number_v, dest_v,
-                local_sem, in_sem, send_sem, recv_sem, ids_send, ids_recv, ret_send, ret_recv,
+                run_out, rows_out, ids_out, ret,
+                raw, nrm, idv, idt, acc, obuf, oid, prior_v, owned_v, number_v, dest_v,
+                local_sem, in_sem, send_sem, recv_sem, block_recv, ids_send, ids_recv, ret_send, ret_recv,
                 rows_send, rows_recv, oids_send, oids_recv, keep_sem, known_sem):
     n_grp, n_blk = sizes
     devices = n_grp * n_blk
@@ -378,8 +373,12 @@
         return 2 * (r + flip * (3 - 2 * r)) + x
 
     def to_device(step):
-        other = (me + step) % devices
-        return other, other // n_blk, other % n_blk
+        turn = (step - 1) // n_blk
+        u = (step - 1) % n_blk + turn // (n_grp - 1)
+        og = (g + u // 2) % n_grp
+        oz = pick(4 * z + turn, [2, 1, 3, 0, 2, 3, 0, 1, 1, 0, 3, 2, 1, 2, 0, 3])
+        ob = 2 * oz + (x + u) % 2
+        return og * n_blk + ob, og, ob
 
     barrier = pltpu.get_barrier_semaphore()
 
@@ -431,6 +430,8 @@
         return pl.ds(pl.multiple_of(k * part, part), part)
 
     def span(c):
+        if isinstance(c, int):
+            return pl.ds(c * ch, ch)
         return pl.ds(pl.multiple_of(c * ch, ch), ch)
 
     whole = pl.ds(0, rows)
@@ -444,17 +445,26 @@
     takes_pair = (role > 0) | (x == 1)
     early = role >= 2
 
-    def own_copy(k):
+    def own_copy(k, sem):
         return remote(emb.at[0, piece(k), :], raw.at[own_slot, piece(k), :],
-                      send_sem.at[0, k], recv_sem.at[own_slot, k], own_to)
+                      send_sem.at[0, k // SPLIT], sem, own_to)
 
     def pair_copy(k):
         return remote(emb.at[0, piece(k), :], raw.at[PAIR, piece(k), :],
-                      send_sem.at[1, k], recv_sem.at[PAIR, k], partner)
+                      send_sem.at[1, k // SPLIT], block_recv.at[0, k // SPLIT], partner)
 
     def onward_copy(s, k):
         return remote(raw.at[s, piece(k), :], raw.at[s, piece(k), :],
-                      send_sem.at[s, k], recv_sem.at[s, k], onward)
+                      send_sem.at[s, k // SPLIT], recv_sem.at[s - ONE, k], onward)
+
+    def sent(lane, c):
+        remote(raw.at[OWN, span(c), :], raw.at[OWN, span(c), :], send_sem.at[lane, c], block_recv.at[0, c], partner).wait_send()
+
+    def send_own(first, last):
+        @pl.when(role < 2)
+        def _():
+            for k in range(first, last):
+                own_copy(k, recv_sem.at[own_slot - ONE, k]).start()
 
     def ids_copy(src, lane, slot, blk):
         return remote(src, idv.at[slot], ids_send.at[lane], ids_recv.at[slot], blk)
@@ -463,18 +473,19 @@
     def _():
         ids_copy(ids, 0, own_slot, own_to).start()
 
-    @pl.when(role < 2)
+    send_own(0, SPLIT)
+
+    @pl.when(role == 0)
+    def _():
+        send_own(SPLIT, pieces)
+
+    @pl.when(gives_pair)
+    def _():
+        ids_copy(ids, 1, PAIR, partner).start()
+
+    @pl.when(early)
     def _():
         for k in range(pieces):
-            own_copy(k).start()
-
-    @pl.when(gives_pair)
-    def _():
-        ids_copy(ids, 1, PAIR, partner).start()
-
-    @pl.when(early)
-    def _():
-        for k in range(LEAD):
             pair_copy(k).start()
 
     def normalize(values):
@@ -598,118 +609,147 @@
         ids_copy(idv.at[s], 1, s, partner).wait_recv()
 
     def stream_wait(s, k):
-        remote(raw.at[s, piece(k), :], raw.at[s, piece(k), :], send_sem.at[1, k], recv_sem.at[s, k], partner).wait_recv()
+        remote(raw.at[s, piece(k), :], raw.at[s, piece(k), :], send_sem.at[1, 0], recv_sem.at[s - ONE, k], partner).wait_recv()
+
+    def block_wait(s, c):
+        remote(raw.at[s, span(c), :], raw.at[s, span(c), :], send_sem.at[1, 0],
+               block_recv.at[int(s == THREE), c], partner).wait_recv()
+
+    def pass_on(s, k):
+        stream_wait(s, k)
+
+        @pl.when(role < 3)
+        def _():
+            onward_copy(s, k).start()
+
+    def pass_ids(s):
+        ids_wait(s)
+
+        @pl.when(role < 3)
+        def _():
+            ids_copy(idv.at[s], s, s, onward).start()
+
+    def take_three(c):
+        @pl.when(c == 0)
+        def _():
+            ids_wait(THREE)
+
+        block_wait(THREE, c)
+        ready(THREE, c)
+
+    @pl.when(role == 2)
+    def _():
+        pass_ids(ONE)
+        for k in range(SPLIT):
+            pass_on(ONE, k)
 
     @pl.loop(0, 2 * CHUNKS)
     def _(p):
         phase = p // CHUNKS
         c = p % CHUNKS
-        has_in = role > phase
-        s_in = jnp.where((phase == 1) | (role == 1), ZERO, ONE)
+        has_in = (role > 0) & ((phase == 0) | (role > 1))
+        s_in = jnp.where(phase == 0, ZERO, ONE)
+        ahead = jnp.where((role == 2) & (phase == 1), 1, 0)
+        c_in = (c + ahead) % CHUNKS
 
         def take(i):
-            k = SPLIT * c + i
-
-            @pl.when(has_in)
+            k = SPLIT * c_in + i
+
+            if i == 0:
+                @pl.when(has_in & (c == 0) & ((role != 2) | (phase == 0)))
+                def _():
+                    pass_ids(s_in)
+
+            @pl.when(has_in & (c + ahead < CHUNKS))
             def _():
-                stream_wait(s_in, k)
-                if i == 0:
-                    @pl.when(c == 0)
-                    def _():
-                        ids_wait(s_in)
-
-                @pl.when(role < 3)
+                pass_on(s_in, k)
+
+            if i == SPLIT - 1:
+                @pl.when((phase == 0) & (role == 0))
                 def _():
-                    onward_copy(s_in, k).start()
-                    if i == 0:
-                        @pl.when(c == 0)
-                        def _():
-                            ids_copy(idv.at[s_in], s_in, s_in, onward).start()
-
-            @pl.when((phase == 0) & (role == 0))
+                    sent(0, c)
+
+            @pl.when((phase == 0) & (role == 3) & (k >= THREE_FROM) & (k < THREE_FROM + pieces // 2))
             def _():
-                own_copy(k).wait_send()
-
-            @pl.when((phase == 0) & early & (k + LEAD < pieces))
-            def _():
-                pair_copy(k + LEAD).start()
-
-            @pl.when((phase == 0) & (role == 3) & (k >= pieces // 2))
-            def _():
-                own_copy(2 * k - pieces).start()
-                own_copy(2 * k - pieces + 1).start()
-
-            if i == 0:
-                @pl.when((phase == 1) & (role < 2) & takes_pair & (c == 0))
-                def _():
-                    ids_wait(PAIR)
-
-            @pl.when((phase == 1) & (role < 2) & takes_pair)
-            def _():
-                stream_wait(PAIR, k)
-
-            @pl.when((phase == 1) & (role == 0) & gives_pair)
-            def _():
-                pair_copy(k).wait_send()
-
-            @pl.when((phase == 1) & (role < 2) & gives_pair & (k + LATE_LEAD < pieces))
-            def _():
-                pair_copy(k + LATE_LEAD).start()
-
-        for i in range(SPLIT // 2):
-            take(i)
+                for n in range(2):
+                    m = 2 * (k - THREE_FROM) + n
+                    own_copy(m, block_recv.at[1, m // SPLIT]).start()
+
+        @pl.when((phase == 1) & (role == 0) & gives_pair & (c > 0))
+        def _():
+            sent(1, c - 1)
+
+        @pl.when((phase == 1) & (role < 2) & gives_pair & (c + LATE_LEAD < CHUNKS))
+        def _():
+            for i in range(SPLIT):
+                pair_copy(SPLIT * (c + LATE_LEAD) + i).start()
+
+        take(0)
+
+        @pl.when((p == 2 * CHUNKS - 1) & (role == 3))
+        def _():
+            start_routing()
+
+        @pl.when((role == 2) & (phase == 1))
+        def _():
+            take_three(c)
+
+        run_units(UNITS[0], phase, c)
+        take(1)
 
         @pl.when((p == LATE_STEP) & (role < 2) & gives_pair)
         def _():
-            for k in range(LATE_LEAD):
+            for k in range(LATE_LEAD * SPLIT):
                 pair_copy(k).start()
 
-        @pl.when((p == 2 * CHUNKS - 1) & (role != 2))
-        def _():
-            start_routing()
-
-        run_units(UNITS_FIRST, phase, c)
-        for i in range(SPLIT // 2, SPLIT):
-            take(i)
-
-        @pl.when((p == 2 * CHUNKS - 1) & (role == 2))
-        def _():
-            start_routing()
-
-        told((p == 0) & (z == 3), 0)
-        told((p == 0) & (z == 0), 1)
-        told(p == 0, None, (2, other_core, b))
-        told(p == 1, 2, (3, other_row, b))
-        told(p == 2, 3)
-
-        @pl.when(has_in)
-        def _():
-            ready(s_in, c)
-
-        @pl.when((phase == 0) & early)
+        run_units(UNITS[1], phase, c)
+        take(2)
+        run_units(UNITS[2], phase, c)
+        take(3)
+
+        @pl.when((phase == 1) & (role < 2) & takes_pair)
         def _():
             @pl.when(c == 0)
             def _():
                 ids_wait(PAIR)
 
-            for i in range(SPLIT):
-                stream_wait(PAIR, SPLIT * c + i)
-
-        @pl.when((early == (phase == 0)) & takes_pair)
-        def _():
-            ready(PAIR, c)
-
-        @pl.when((role == 2) & (phase == 1))
+            block_wait(PAIR, c)
+
+        @pl.when((p == 2 * CHUNKS - 1) & (role == 0) & gives_pair)
+        def _():
+            sent(1, c)
+
+        @pl.when((role < 3) & (p == jnp.where(role == 2, 2 * CHUNKS - 2, 2 * CHUNKS - 1)))
+        def _():
+            start_routing()
+
+        @pl.when((p == CHUNKS - 1) & (role == 1))
+        def _():
+            send_own(SPLIT, pieces)
+
+        told((p == 0) & (z == 3), 0)
+        told((p == 0) & (z == 0), 1)
+        told(p == 1, None, (2, other_core, b))
+        told(p == 3, 2, (3, other_row, b))
+        told(p == 4, 3)
+
+        @pl.when(has_in)
+        def _():
+            ready(s_in, c_in)
+
+        @pl.when((phase == 0) & early)
         def _():
             @pl.when(c == 0)
             def _():
-                ids_wait(THREE)
-
-            for i in range(SPLIT):
-                stream_wait(THREE, SPLIT * c + i)
-            ready(THREE, c)
-
-        run_units(UNITS_SECOND, phase, c)
+                ids_wait(PAIR)
+
+            block_wait(PAIR, c)
+
+        @pl.when((early == (phase == 0)) & takes_pair)
+        def _():
+            ready(PAIR, c)
+
+        run_units(UNITS[3], phase, c_in)
 
     def back(slot, index, r):
         return remote(acc.at[slot], ret.at[index], ret_send.at[slot], ret_recv.at[index],
@@ -722,14 +762,17 @@
         def _(slot=slot, index=index, r=r):
             back(slot, index, r).start()
 
+    own_result = pltpu.make_async_copy(acc.at[OWN], run_out, keep_sem.at[2])
+    own_result.start()
+
     @pl.when(gives_pair)
     def _():
         ids_copy(ids, 1, PAIR, partner).wait_send()
 
     @pl.when(role > 0)
     def _():
-        for k in range(pieces):
-            pair_copy(k).wait_send()
+        for c in range(CHUNKS):
+            sent(1, c)
 
     @pl.when(has_own)
     def _():
@@ -737,16 +780,17 @@
 
     @pl.when((role == 1) | (role == 3))
     def _():
-        for k in range(pieces):
-            own_copy(k).wait_send()
+        for c in range(CHUNKS):
+            sent(0, c)
 
     for s, sends in ((ONE, role == 2), (ZERO, (role == 1) | (role == 2))):
         @pl.when(sends)
         def _(s=s):
             ids_copy(idv.at[s], s, s, onward).wait_send()
-            for k in range(pieces):
-                onward_copy(s, k).wait_send()
-
+            for c in range(CHUNKS):
+                sent(s, c)
+
+    own_result.wait()
     keep_rows.wait()
     keep_ids.wait()
     others = pl.ds(0, devices - 1)
@@ -755,12 +799,10 @@
     pltpu.make_async_copy(obuf.at[others], rows_out.at[others], rows_recv).wait()
     pltpu.make_async_copy(oid.at[others], ids_out.at[others], oids_recv).wait()
 
-    run_out[...] = acc[OWN]
     for index, gets in enumerate((role > 0, role == 0, (role != 2), role < 2)):
         @pl.when(gets)
         def _(index=index):
             remote(acc.at[PAIR], ret.at[index], ret_send.at[PAIR], ret_recv.at[index], partner).wait_recv()
-            run_out[...] = jnp.maximum(run_out[...], ret[index])
 
     for when, slot, index, r in returns:
         @pl.when(when)
@@ -768,8 +810,18 @@
             back(slot, index, r).wait_send()
 
 
-def place_kernel(run, routed, routed_ids, run_out, rows_out, ids_out):
-    run_out[...] = run[...]
+def place_kernel(line, run, routed, routed_ids, *rest):
+    if line:
+        ret, run_out, rows_out, ids_out = rest
+        z = lax.axis_index("blk") // 2
+        role = z + (lax.axis_index("grp") % 2) * (3 - 2 * z)
+        result = run[...]
+        for index, gets in enumerate((role > 0, role == 0, role != 2, role < 2)):
+            result = jnp.maximum(result, jnp.where(gets, ret[index], EMPTY))
+        run_out[...] = result
+    else:
+        run_out, rows_out, ids_out = rest
+        run_out[...] = run[...]
     devices, cap, _ = routed.shape
     for d in range(0, devices, 2):
         both = jnp.concatenate([routed[d].astype(jnp.float32), routed[d + 1].astype(jnp.float32)], axis=0)
@@ -802,25 +854,24 @@
         slots, pieces = 5, SPLIT * CHUNKS
         results = pl.pallas_call(
             functools.partial(line_kernel, (n_grp, n_blk)),
-            out_shape=shapes,
+            out_shape=shapes + (jax.ShapeDtypeStruct((4, 1, rows), jnp.float32),),
             in_specs=[anywhere] * 6,
-            out_specs=(vmem, anywhere, anywhere),
+            out_specs=(anywhere,) * 4,
             scratch_shapes=[
                 pltpu.VMEM((slots, rows, width), jnp.bfloat16),
                 pltpu.VMEM((slots, rows, width), jnp.bfloat16),
                 pltpu.VMEM((slots, 1, rows), jnp.int32),
                 pltpu.VMEM((slots, rows, LANES), jnp.float32),
                 pltpu.VMEM((slots, 1, rows), jnp.float32),
-                pltpu.VMEM((4, 1, rows), jnp.float32),
                 pltpu.VMEM((devices, CAP, width), jnp.bfloat16),
                 pltpu.VMEM((devices, 1, LANES), jnp.int32),
                 pltpu.VMEM((1, rows), jnp.float32),
                 pltpu.VMEM((own_dev, width), jnp.bfloat16),
                 pltpu.VMEM((1, own_dev), jnp.int32),
                 pltpu.VMEM((1, own_dev), jnp.int32),
-                dma, dma((5,)), dma((slots, pieces)), dma((slots, pieces)),
+                dma, dma((5,)), dma((4, CHUNKS)), dma((2, pieces)), dma((2, CHUNKS)),
                 dma((slots,)), dma((slots,)), dma((slots,)), dma((4,)),
-                dma, dma, dma, dma, dma((2,)), pltpu.SemaphoreType.REGULAR((4,)),
+                dma, dma, dma, dma, dma((3,)), pltpu.SemaphoreType.REGULAR((4,)),
             ],
             compiler_params=pltpu.CompilerParams(has_side_effects=True, collective_id=0, vmem_limit_bytes=limit),
         )(embeds, doc_ids, prior_max, owned, owned_ids.reshape(1, own_dev), owner_dest.reshape(1, own_dev))
@@ -850,13 +901,13 @@
             compiler_params=pltpu.CompilerParams(has_side_effects=True, vmem_limit_bytes=limit),
         )(embeds, doc_ids, prior_max, owned, owned_ids.reshape(1, own_dev), owner_dest)
     running, next_rows, next_ids = pl.pallas_call(
-        place_kernel,
+        functools.partial(place_kernel, line),
         out_shape=(
             jax.ShapeDtypeStruct((1, rows), jnp.float32),
             jax.ShapeDtypeStruct((devices * CAP, width), jnp.bfloat16),
             jax.ShapeDtypeStruct((1, devices * CAP), jnp.int32),
         ),
-        in_specs=[vmem] * 3,
+        in_specs=[vmem] * len(results),
         out_specs=(vmem,) * 3,
     )(*results)
     return (running, next_rows, next_ids.reshape(devices * CAP))

time: 71.2 us -> 67.8 us (0.952)
  Pallas kernels: 70.4 us -> 67 us
    pallas_call x1, Pallas kernels: 68.7 us -> 65.3 us  [body(): pl.pallas_call(functools.partial(line_kernel, (n_grp, n_blk)), out_shape=...]
where the time goes in v3:
time: 67.8 us; the launch traced here: 67.6 us
  Pallas kernels  67 us (99%)
    pallas_call x1, Pallas kernels, body(): pl.pallas_call(functools.partial(line_kernel, (n_grp, n_blk)), out_shape=...  65.3 us
    pallas_call x1, Pallas kernels, body(): pl.pallas_call(functools.partial(place_kernel, line), out_shape=(jax.Shap...  1.72 us

profile of v3, /device:TPU:0, one launch (start us, length us, event | category | flops | bytes accessed | tf_op | source)
XLA Modules:
  0.0 67.6 jit_solution(7030785820696518251)
XLA Ops:
  0.6 65.3 %shard_map.85 = (f32[1,1024]{1,0:T(1,128)}, bf16[32,4,1024]{2,1,0:T(4,128)(2,1)}, s32[32,1,128]{2,1,0:T(1,128)}, f32[4,1,1024]{2,1,0:T(1,128)}) custom-call(bf16[1,1024,1024]{2,1,0:T(8,128)(2,1)} %emb.1, s32[1,1024]{1,0:T(1,128)} %ids.1, f32[1,1024]{1,0:T(1,128)} %prior.1, bf16[64,1024]{1,0:T(8,128)(2,1)} %owned.1, s32[1,64]{1,0:T(1,128)} %bitcast.3, ...), custom_call_target="tpu_custom_call" | custom-call | tf_op jit(solution)/shard_map/pallas_call | solution.py:855
  65.9 1.7 %shard_map.86 = (f32[1,1024]{1,0:T(1,128)}, bf16[128,1024]{1,0:T(8,128)(2,1)}, s32[1,128]{1,0:T(1,128)}) custom-call(f32[1,1024]{1,0:T(1,128)} %get-tuple-element.10.run, bf16[32,4,1024]{2,1,0:T(4,128)(2,1)} %get-tuple-element.11.routed, s32[32,1,128]{2,1,0:T(1,128)} %get-tuple-element.12.routed_ids, f32[4,1,1024]{2,1,0:T(1,128)} %get-tuple-element.13.rest_0_), custom_call_target="tpu_custom_call" | custom-call | tf_op jit(solution)/shard_map/pallas_call | solution.py:903

commit v4 on v3

--- a/solution.py
+++ b/solution.py
@@ -341,12 +341,18 @@
 OWN, PAIR, ONE, ZERO, THREE = range(5)
 SELF_UNIT = (OWN, OWN)
 OWN_PAIR = (PAIR, OWN)
+KINDS = 3
 UNITS = (
-    (((), ()), ((), ()), ((), ((THREE, OWN),)), ((), ())),
-    (((SELF_UNIT,), ()), ((SELF_UNIT,), ()), ((SELF_UNIT,), ((ZERO, PAIR),)), ((SELF_UNIT,), ((ZERO, PAIR),))),
-    (((), ()), ((), ()), ((), ((THREE, PAIR),)), ((), ())),
-    (((), (OWN_PAIR,)), (((ZERO, OWN),), ((PAIR, ZERO), OWN_PAIR)),
-     ((OWN_PAIR,), ((ONE, OWN), (ONE, PAIR))), (((ZERO, OWN), OWN_PAIR), ((ONE, PAIR),))),
+    (((), (), ()), ((), (), ()),
+     ((), ((THREE, OWN),), ((ONE, OWN), (ONE, PAIR))), ((), (), ())),
+    (((SELF_UNIT,), (), ()), ((SELF_UNIT,), (), ()),
+     ((SELF_UNIT,), ((ZERO, PAIR),), ((ZERO, PAIR),)), ((SELF_UNIT,), ((ZERO, PAIR),), ((ZERO, PAIR),))),
+    (((), (), ()), ((), (), ()),
+     ((), ((THREE, PAIR),), ((THREE, OWN),)), ((), (), ())),
+    (((), (OWN_PAIR,), (OWN_PAIR,)),
+     (((ZERO, OWN),), ((PAIR, ZERO), OWN_PAIR), ((PAIR, ZERO), OWN_PAIR)),
+     ((OWN_PAIR,), ((ONE, OWN), (ONE, PAIR)), ((THREE, PAIR),)),
+     (((ZERO, OWN), OWN_PAIR), ((ONE, PAIR),), ((ONE, PAIR),))),
 )
 
 
@@ -373,10 +379,11 @@
         return 2 * (r + flip * (3 - 2 * r)) + x
 
     def to_device(step):
-        turn = (step - 1) // n_blk
-        u = (step - 1) % n_blk + turn // (n_grp - 1)
+        place = step - 1 + jnp.where(step > 2 * n_blk, 1, 0)
+        turn = place // n_blk
+        u = place % n_blk
         og = (g + u // 2) % n_grp
-        oz = pick(4 * z + turn, [2, 1, 3, 0, 2, 3, 0, 1, 1, 0, 3, 2, 1, 2, 0, 3])
+        oz = pick(4 * z + turn, [3, 2, 0, 1, 3, 2, 1, 0, 0, 1, 2, 3, 0, 1, 3, 2])
         ob = 2 * oz + (x + u) % 2
         return og * n_blk + ob, og, ob
 
@@ -559,15 +566,19 @@
     keep_rows = pltpu.make_async_copy(obuf.at[me], rows_out.at[me], keep_sem.at[0])
     keep_ids = pltpu.make_async_copy(oid.at[me], ids_out.at[me], keep_sem.at[1])
 
-    def start_routing():
+    def start_routing(upward):
         @pl.loop(1, devices)
         def _(step):
             other, og, ob = to_device(step)
-            remote(obuf.at[other], rows_out.at[me], rows_send, rows_recv, ob, og).start()
-            remote(oid.at[other], ids_out.at[me], oids_send, oids_recv, ob, og).start()
-
-        keep_rows.start()
-        keep_ids.start()
+
+            @pl.when((ob // 2 > z) == upward)
+            def _():
+                remote(obuf.at[other], rows_out.at[me], rows_send, rows_recv, ob, og).start()
+                remote(oid.at[other], ids_out.at[me], oids_send, oids_recv, ob, og).start()
+
+        if not upward:
+            keep_rows.start()
+            keep_ids.start()
 
     def is_row(u, v):
         diff = (u - v + n_blk) % n_blk
@@ -581,10 +592,10 @@
             result = jnp.where(slot == i, slot_blocks[i], result)
         return result
 
-    def run_units(table, phase, c):
+    def run_units(table, kind, c):
         longest = max(len(entry) for by_phase in table for entry in by_phase)
         lists = [entry for by_phase in table for entry in by_phase]
-        which_list = role * 2 + phase
+        which_list = role * KINDS + kind
         ends = [int(len(entry) > 0 and entry[-1] == OWN_PAIR) for entry in lists]
         count = pick(which_list, [len(entry) for entry in lists]) - pick(which_list, ends) * (1 - x)
 
@@ -615,6 +626,10 @@
         remote(raw.at[s, span(c), :], raw.at[s, span(c), :], send_sem.at[1, 0],
                block_recv.at[int(s == THREE), c], partner).wait_recv()
 
+    def back(slot, index, r):
+        return remote(acc.at[slot], ret.at[index], ret_send.at[slot], ret_recv.at[index],
+                      partner if r is None else block_of(r))
+
     def pass_on(s, k):
         stream_wait(s, k)
 
@@ -642,6 +657,7 @@
         pass_ids(ONE)
         for k in range(SPLIT):
             pass_on(ONE, k)
+        ready(ONE, jnp.int32(0))
 
     @pl.loop(0, 2 * CHUNKS)
     def _(p):
@@ -651,6 +667,8 @@
         s_in = jnp.where(phase == 0, ZERO, ONE)
         ahead = jnp.where((role == 2) & (phase == 1), 1, 0)
         c_in = (c + ahead) % CHUNKS
+        last = p == 2 * CHUNKS - 1
+        kind = phase + jnp.where(last, 1, 0)
 
         def take(i):
             k = SPLIT * c_in + i
@@ -688,13 +706,18 @@
 
         @pl.when((p == 2 * CHUNKS - 1) & (role == 3))
         def _():
-            start_routing()
+            start_routing(False)
 
         @pl.when((role == 2) & (phase == 1))
         def _():
             take_three(c)
 
-        run_units(UNITS[0], phase, c)
+        run_units(UNITS[0], kind, jnp.where(last, c_in, c))
+
+        @pl.when(last & (role == 2))
+        def _():
+            back(ONE, 2, 1).start()
+
         take(1)
 
         @pl.when((p == LATE_STEP) & (role < 2) & gives_pair)
@@ -702,9 +725,15 @@
             for k in range(LATE_LEAD * SPLIT):
                 pair_copy(k).start()
 
-        run_units(UNITS[1], phase, c)
+        run_units(UNITS[1], kind, c)
+
+        @pl.when((p == 2 * CHUNKS - 1) & early)
+        def _():
+            back(ZERO, role, 0).start()
+            start_routing(True)
+
         take(2)
-        run_units(UNITS[2], phase, c)
+        run_units(UNITS[2], kind, c)
         take(3)
 
         @pl.when((phase == 1) & (role < 2) & takes_pair)
@@ -721,7 +750,7 @@
 
         @pl.when((role < 3) & (p == jnp.where(role == 2, 2 * CHUNKS - 2, 2 * CHUNKS - 1)))
         def _():
-            start_routing()
+            start_routing(False)
 
         @pl.when((p == CHUNKS - 1) & (role == 1))
         def _():
@@ -733,7 +762,7 @@
         told(p == 3, 2, (3, other_row, b))
         told(p == 4, 3)
 
-        @pl.when(has_in)
+        @pl.when(has_in & (c + ahead < CHUNKS))
         def _():
             ready(s_in, c_in)
 
@@ -749,18 +778,24 @@
         def _():
             ready(PAIR, c)
 
-        run_units(UNITS[3], phase, c_in)
-
-    def back(slot, index, r):
-        return remote(acc.at[slot], ret.at[index], ret_send.at[slot], ret_recv.at[index],
-                      partner if r is None else block_of(r))
+        run_units(UNITS[3], kind, jnp.where(last, c, c_in))
 
     returns = [(role > 0, PAIR, 0, None), (role == 1, ZERO, 1, 0), (role == 2, ZERO, 2, 0), (role == 3, ZERO, 3, 0),
                (role == 2, ONE, 2, 1), (role == 3, ONE, 3, 1), (role == 2, THREE, 2, 3)]
     for when, slot, index, r in reversed(returns):
+        if (slot == ZERO and index > 1) or (slot, index) == (ONE, 2):
+            continue
+
         @pl.when(when)
         def _(slot=slot, index=index, r=r):
             back(slot, index, r).start()
+
+    def returned(index):
+        remote(acc.at[PAIR], ret.at[index], ret_send.at[PAIR], ret_recv.at[index], partner).wait_recv()
+
+    @pl.when(role < 2)
+    def _():
+        start_routing(True)
 
     own_result = pltpu.make_async_copy(acc.at[OWN], run_out, keep_sem.at[2])
     own_result.start()
@@ -799,10 +834,10 @@
     pltpu.make_async_copy(obuf.at[others], rows_out.at[others], rows_recv).wait()
     pltpu.make_async_copy(oid.at[others], ids_out.at[others], oids_recv).wait()
 
-    for index, gets in enumerate((role > 0, role == 0, (role != 2), role < 2)):
+    for index, gets in ((0, role > 0), (1, role == 0), (2, role != 2), (3, role < 2)):
         @pl.when(gets)
         def _(index=index):
-            remote(acc.at[PAIR], ret.at[index], ret_send.at[PAIR], ret_recv.at[index], partner).wait_recv()
+            returned(index)
 
     for when, slot, index, r in returns:
         @pl.when(when)

time: 67.8 us -> 64.9 us (0.957)
  Pallas kernels: 67 us -> 63.5 us
    pallas_call x1, Pallas kernels: 65.3 us -> 61.8 us  [body(): pl.pallas_call(functools.partial(line_kernel, (n_grp, n_blk)), out_shape=...]
where the time goes in v4:
time: 64.9 us; the launch traced here: 64.1 us
  Pallas kernels  63.5 us (98%)
    pallas_call x1, Pallas kernels, body(): pl.pallas_call(functools.partial(line_kernel, (n_grp, n_blk)), out_shape=...  61.8 us
    pallas_call x1, Pallas kernels, body(): pl.pallas_call(functools.partial(place_kernel, line), out_shape=(jax.Shap...  1.72 us

profile of v4, /device:TPU:0, one launch (start us, length us, event | category | flops | bytes accessed | tf_op | source)
XLA Modules:
  0.0 64.1 jit_solution(7250765123283616251)
XLA Ops:
  0.6 61.8 %shard_map.85 = (f32[1,1024]{1,0:T(1,128)}, bf16[32,4,1024]{2,1,0:T(4,128)(2,1)}, s32[32,1,128]{2,1,0:T(1,128)}, f32[4,1,1024]{2,1,0:T(1,128)}) custom-call(bf16[1,1024,1024]{2,1,0:T(8,128)(2,1)} %emb.1, s32[1,1024]{1,0:T(1,128)} %ids.1, f32[1,1024]{1,0:T(1,128)} %prior.1, bf16[64,1024]{1,0:T(8,128)(2,1)} %owned.1, s32[1,64]{1,0:T(1,128)} %bitcast.3, ...), custom_call_target="tpu_custom_call" | custom-call | tf_op jit(solution)/shard_map/pallas_call | solution.py:890
  62.4 1.7 %shard_map.86 = (f32[1,1024]{1,0:T(1,128)}, bf16[128,1024]{1,0:T(8,128)(2,1)}, s32[1,128]{1,0:T(1,128)}) custom-call(f32[1,1024]{1,0:T(1,128)} %get-tuple-element.10.run, bf16[32,4,1024]{2,1,0:T(4,128)(2,1)} %get-tuple-element.11.routed, s32[32,1,128]{2,1,0:T(1,128)} %get-tuple-element.12.routed_ids, f32[4,1,1024]{2,1,0:T(1,128)} %get-tuple-element.13.rest_0_), custom_call_target="tpu_custom_call" | custom-call | tf_op jit(solution)/shard_map/pallas_call | solution.py:938

commit v5 on v4

--- a/solution.py
+++ b/solution.py
@@ -335,9 +335,9 @@
 
 
 SPLIT = 4
-LATE_LEAD = 2
+LATE_LEAD = 3
 LATE_STEP = 3
-THREE_FROM = 7
+THREE_FROM = 6
 OWN, PAIR, ONE, ZERO, THREE = range(5)
 SELF_UNIT = (OWN, OWN)
 OWN_PAIR = (PAIR, OWN)

time: 64.9 us -> 64.9 us (level)
  no operation moved by 1% of the time
where the time goes in v5:
time: 64.9 us; the launch traced here: 64.1 us
  Pallas kernels  63.5 us (98%)
    pallas_call x1, Pallas kernels, body(): pl.pallas_call(functools.partial(line_kernel, (n_grp, n_blk)), out_shape=...  61.8 us
    pallas_call x1, Pallas kernels, body(): pl.pallas_call(functools.partial(place_kernel, line), out_shape=(jax.Shap...  1.72 us

profile of v5, /device:TPU:0, one launch (start us, length us, event | category | flops | bytes accessed | tf_op | source)
XLA Modules:
  0.0 64.1 jit_solution(7474467624670722110)
XLA Ops:
  0.6 61.8 %shard_map.85 = (f32[1,1024]{1,0:T(1,128)}, bf16[32,4,1024]{2,1,0:T(4,128)(2,1)}, s32[32,1,128]{2,1,0:T(1,128)}, f32[4,1,1024]{2,1,0:T(1,128)}) custom-call(bf16[1,1024,1024]{2,1,0:T(8,128)(2,1)} %emb.1, s32[1,1024]{1,0:T(1,128)} %ids.1, f32[1,1024]{1,0:T(1,128)} %prior.1, bf16[64,1024]{1,0:T(8,128)(2,1)} %owned.1, s32[1,64]{1,0:T(1,128)} %bitcast.3, ...), custom_call_target="tpu_custom_call" | custom-call | tf_op jit(solution)/shard_map/pallas_call | solution.py:890
  62.4 1.7 %shard_map.86 = (f32[1,1024]{1,0:T(1,128)}, bf16[128,1024]{1,0:T(8,128)(2,1)}, s32[1,128]{1,0:T(1,128)}) custom-call(f32[1,1024]{1,0:T(1,128)} %get-tuple-element.10.run, bf16[32,4,1024]{2,1,0:T(4,128)(2,1)} %get-tuple-element.11.routed, s32[32,1,128]{2,1,0:T(1,128)} %get-tuple-element.12.routed_ids, f32[4,1,1024]{2,1,0:T(1,128)} %get-tuple-element.13.rest_0_), custom_call_target="tpu_custom_call" | custom-call | tf_op jit(solution)/shard_map/pallas_call | solution.py:938
